TPU v7x, 512 devices: a whole 4x8x8 slice. The times are simulated.
512 devices in a mesh: seq: 64 (over z, x, core), tp: 8 (over y).
Axes of the slice: x: 4, y: 8, z: 8, core: 2. Of those that a mesh axis runs over, the one named last changes fastest.
Arguments:
- hidden_in: bfloat16 [8192, 4096], P('seq', 'tp'), may hold values from -64 to 64
- span_order: int32 [64], replicated, may hold values from 0 to 63, each once
- norm_gain: bfloat16 [4096], P('tp'), may hold values from 0.099609375 to 1.8984375
- w_query: bfloat16 [4096, 4096], P('seq', 'tp'), may hold values from -0.09375 to 0.09375
- bias_query: bfloat16 [4096], P('tp'), may hold values from -14 to 14
- key_value_weight: bfloat16 [4096, 2, 1024], P('seq', None, 'tp'), may hold values from -0.09375 to 0.09375
- bias_kv: bfloat16 [2, 1024], P(None, 'tp'), may hold values from -14 to 14
- w_out: bfloat16 [4096, 4096], P('tp', 'seq'), may hold values from -0.09375 to 0.09375
- post_gain: bfloat16 [4096], P('tp'), may hold values from 0.099609375 to 1.8984375
Outputs:
- attn_out: bfloat16 [8192, 4096], P('seq', 'tp')
- normed: bfloat16 [8192, 4096], P('seq', 'tp')
Inputs may be any that keep to these rules, and one draw needn't show every extreme that they name: Each span number appears once; row r of hidden_in belongs to span span_order[r // 128].
All inputs are finite; a program needn't handle non-finite values.
Results may differ from a plain program's by a relative error of at most 0.014.
Values may be sent and summed in bfloat16 or wider, within the bound.
No kernel may reach another device: no remote copies, remote signals or barrier semaphores. Data moves between devices by JAX's collectives and lax.ppermute only.
A program may use at most 64 MiB of HBM per device.

v0:
```python
import functools
import math

import jax
import jax.numpy as jnp
from jax import lax
from jax.experimental import pallas as pl
from jax.experimental.pallas import tpu as pltpu
from jax.sharding import Mesh
from jax.sharding import PartitionSpec as P


MODEL_WIDTH = 4096
HEAD = 128
TOK = 128
GROUP = 4
NZ, NX, NC, NY = 8, 4, 2, 8
SEQ = ("z", "x", "c")
TP = ("tq", "tr")
EPS = 1e-06
ROPE_BASE = 1000000.0
NEG = -(2.0**100)
F32 = jnp.float32
BF16 = jnp.bfloat16


def call(kernel, outs, *args, scratch=(), kept=(), free=(), far=(), limit=24):
    specs, given = [], []
    for k, a in enumerate(args):
        if a.dtype == jnp.int32:
            specs.append(pl.BlockSpec(memory_space=pltpu.SMEM))
        else:
            specs.append(pl.BlockSpec(memory_space=pltpu.VMEM))
            if k not in free:
                space = pltpu.HBM if k in far else pltpu.VMEM
                a = pltpu.with_memory_space_constraint(a, space)
        given.append(a)
    shapes = [
        jax.ShapeDtypeStruct(s, d) if k in kept else pltpu.VMEM(s, d)
        for k, (s, d) in enumerate(outs)
    ]
    spec = [pl.BlockSpec(memory_space=pltpu.VMEM)] * len(outs)
    return pl.pallas_call(
        kernel,
        out_shape=shapes,
        in_specs=specs,
        out_specs=spec,
        scratch_shapes=list(scratch),
        compiler_params=pltpu.CompilerParams(vmem_limit_bytes=limit << 20),
    )(*given)


def split_sum(value):
    high = value.astype(BF16).astype(F32)
    rest = value - high
    middle = rest.astype(BF16).astype(F32)
    return high, middle, (rest - middle)


def rows_of(terms, count):
    width = terms[0].shape[1]
    ids = lax.broadcasted_iota(jnp.int32, (count, width), 0)
    out = jnp.zeros((count, width), F32)
    for k, term in enumerate(terms):
        out = jnp.where(ids == k, jnp.broadcast_to(term, (count, width)), out)
    return out.astype(BF16)


def row_sums(square):
    part = square[:, 0:128] + square[:, 128:256] + square[:, 256:384] + square[:, 384:512]
    return jnp.sum(part.T, axis=0, keepdims=True)


def prepare(h_ref, g_ref, p_ref):
    h = h_ref[...].astype(F32)
    tail = rows_of(split_sum(row_sums(h * h)), 8)
    scaled = (h * g_ref[...].astype(F32).reshape(1, 512)).T
    for x in range(NX):
        block = scaled[x * 128 : (x + 1) * 128, :].astype(BF16)
        for y in range(NY):
            p_ref[x * NY + y, 0:128, :] = block
            p_ref[x * NY + y, 128:136, :] = tail


def stack_weights(wq_ref, wkv_ref, wo_ref, w_ref):
    w_ref[:, 0:512] = wq_ref[...]
    w_ref[:, 512:640] = wkv_ref[:, 0, :]
    w_ref[:, 640:768] = wkv_ref[:, 1, :]
    w_ref[:, 768:1280] = wo_ref[...]


def sources(z, c):
    sign = 2 * c - 1
    near = [z] + [z + sign * k for k in (1, 2, 3, 4)] + [z - sign * k for k in (1, 2, 3)]
    return [(n + NZ) & (NZ - 1) for n in near]


def project(x_ref, *refs):
    w_refs, (out_ref, xs_ref) = refs[:8], refs[8:]
    c = lax.axis_index("c")
    at = sources(lax.axis_index("z"), c)
    scales = []
    for x in range(NX):
        total = jnp.zeros((1, 128), F32)
        for y in range(NY):
            tail = x_ref[x * NY + y, 128:136, :].astype(F32)
            total += tail[0:1] + tail[1:2] + tail[2:3]
        scales.append(lax.rsqrt(total / MODEL_WIDTH + EPS))
    scale = jnp.concatenate(scales, axis=1)
    for k in range(8):
        for x in range(NX):
            block = x_ref[pl.ds(x * NY + at[k], 1), 0:128, :].reshape(128, 128)
            xs_ref[k * 128 : (k + 1) * 128, x * 128 : (x + 1) * 128] = block
    weights = jnp.concatenate([w[...] for w in w_refs], axis=0)
    out = lax.dot_general(
        weights, xs_ref[...], (((0,), (0,)), ((), ())), preferred_element_type=F32
    )
    out = (out * scale).astype(BF16)
    for x in range(NX):
        out_ref[x] = out[:, x * 128 : (x + 1) * 128]


def rotate(r_ref, b_ref, cos_ref, sin_ref, q_ref, kv_ref):
    def total(low, high):
        out = b_ref[low:high, :]
        for x in range(NX):
            out = out + r_ref[x, low:high, :].astype(F32)
        return out

    cos, sin = cos_ref[...], sin_ref[...]

    def turned(head):
        first = total(head * 128, head * 128 + 64)
        second = total(head * 128 + 64, head * 128 + 128)
        return jnp.concatenate(
            [first * cos - second * sin, second * cos + first * sin], axis=0
        )

    for head in range(GROUP):
        q_ref[:, head * 128 : (head + 1) * 128] = turned(head).astype(BF16)
    key = turned(GROUP).T.astype(BF16)
    value = total(640, 768).astype(BF16)
    for z in range(NZ):
        kv_ref[z, 0:128, :] = key
        kv_ref[z, 128:256, :] = value


def attend(order_ref, q0, q1, q2, q3, kv0, kv1, o_ref, s_ref, p_ref):
    z, x, c = (lax.axis_index(a) for a in SEQ)
    key_spans = [order_ref[k * 8 + x * 2 + c] for k in range(NZ)]
    key_spans += [order_ref[k * 8 + x * 2 + 1 - c] for k in range(NZ)]
    values = jnp.concatenate(
        [kv[k, 128:256, :] for kv in (kv0, kv1) for k in range(NZ)], axis=1
    )
    gap = lax.broadcasted_iota(jnp.int32, (128, 512), 0) - (
        lax.broadcasted_iota(jnp.int32, (128, 512), 1) & 127
    )
    factor = math.log2(math.e) / math.sqrt(HEAD)
    for step, q in ((0, q0), (3, q1), (1, q2), (2, q3)):
        owner = (x + step) & 3
        span = order_ref[z * 8 + owner * 2 + c]
        queries = q[...]
        top = jnp.full((8, 512), NEG, F32)
        for k in range(16):
            kv = kv0 if k < 8 else kv1
            s = jnp.dot(kv[k % 8, 0:128, :], queries, preferred_element_type=F32)
            s = jnp.where(gap <= (span - key_spans[k]) * TOK, s * factor, NEG)
            s_ref[k * 128 : (k + 1) * 128, :] = s
            top = jnp.maximum(top, jnp.max(s.reshape(16, 8, 512), axis=0))
        high, low, _ = split_sum(jnp.max(top, axis=0, keepdims=True))
        low = low.astype(BF16).astype(F32)
        peak = high + low
        sums = jnp.zeros((8, 512), F32)
        for k in range(16):
            p = jnp.exp2(s_ref[k * 128 : (k + 1) * 128, :] - peak)
            sums = sums + jnp.sum(p.reshape(16, 8, 512), axis=0)
            p_ref[k * 128 : (k + 1) * 128, :] = p.astype(BF16)
        out = jnp.dot(values, p_ref[...], preferred_element_type=F32)
        total = split_sum(jnp.sum(sums, axis=0, keepdims=True))
        o_ref[pl.ds(owner, 1), 0:128, :] = out.astype(BF16)[None]
        o_ref[pl.ds(owner, 1), 128:144, :] = rows_of((high, low) + total, 16)[None]


def same_parity():
    return (lax.axis_index("z") & 1) == lax.axis_index("tr")


def pick(h1, h2, h3, out_ref):
    late = jnp.logical_and(same_parity(), lax.axis_index("c") == 1)

    @pl.when(late)
    def _():
        out_ref[0:256, :] = h2[...]
        out_ref[256:512, :] = h3[...]

    @pl.when(jnp.logical_not(late))
    def _():
        out_ref[0:256, :] = h1[...]
        out_ref[256:512, :] = h2[...]


def tables(bq_ref, bkv_ref, b_ref):
    for k in range(4):
        row = bq_ref[:, k * 128 : (k + 1) * 128].astype(F32)
        b_ref[k * 128 : (k + 1) * 128, :] = jnp.broadcast_to(row, (128, 128)).T
    for k in range(2):
        row = bkv_ref[k : k + 1, :].astype(F32)
        b_ref[512 + k * 128 : 640 + k * 128, :] = jnp.broadcast_to(row, (128, 128)).T


def merge(o_ref, a_ref):
    tails = [o_ref[k, 128:144, :].astype(F32) for k in range(NX)]
    peaks = [t[0:1] + t[1:2] for t in tails]
    top = functools.reduce(jnp.maximum, peaks)
    shares = [jnp.exp2(peak - top) for peak in peaks]
    total = sum(s * (t[2:3] + t[3:4] + t[4:5]) for s, t in zip(shares, tails))
    out = sum(s * o_ref[k, 0:128, :].astype(F32) for k, s in enumerate(shares)) / total
    out = out.astype(BF16)
    for head in range(GROUP):
        a_ref[head * 128 : (head + 1) * 128, :] = out[:, head * 128 : (head + 1) * 128]


def project_out(a_own, a_other, *refs):
    w_refs, (out_ref, a_ref) = refs[:8], refs[8:]
    z, x, c = (lax.axis_index(a) for a in SEQ)
    side = lax.axis_index("tr")
    a_ref[pl.ds(side, 1)] = a_own[...][None]
    a_ref[pl.ds(1 - side, 1)] = a_other[...][None]
    attended = a_ref[...].reshape(1024, 128)
    same = jnp.where(same_parity(), 1, 0)
    low, high = z - 1 + same, z + 1 + same
    for core in range(2):
        rows = []
        for k in range(4):
            w = w_refs[core * 4 + k]
            for n in range(2):
                at = n * 256
                rows.append(jnp.concatenate([w[at : at + 128, :], w[at + 128 : at + 256, :]], axis=1))
        part = jnp.dot(
            jnp.concatenate(rows, axis=0), attended, preferred_element_type=F32
        ).astype(BF16)
        for k in range(4):
            owner = (x + (0, 3, 1, 2)[k]) & 3
            cols = pl.ds(pl.multiple_of(owner * 128, 128), 128)
            for n in range(2):
                block = jnp.where(c == core, low - 2 * n, high + 2 * n)
                y = ((block + NZ) & (NZ - 1)) >> 1
                at = (k * 2 + n) * 128
                out_ref[pl.ds(y, 1), cols, :] = part[at : at + 128, :][None]


def copied(in_ref, out_ref):
    out_ref[...] = in_ref[...].astype(F32)


def spread(in_ref, out_ref):
    out_ref[...] = jnp.broadcast_to(in_ref[...], (8, 512))


def mix(part_ref, h_ref, attn_ref, stream_ref, sq_ref):
    mixed = part_ref[0].astype(F32)
    for y in range(1, NY // 2):
        mixed = mixed + part_ref[y].astype(F32)
    mixed = mixed.T
    attn_ref[...] = mixed.astype(BF16)
    stream = h_ref[...] + mixed
    stream_ref[...] = stream
    sums = row_sums(stream * stream)
    for y in range(NY):
        sq_ref[y] = sums


def finish(stream_ref, sq_ref, g_ref, out_ref):
    total = sq_ref[0]
    for y in range(1, NY):
        total = total + sq_ref[y]
    scale = lax.rsqrt(total / MODEL_WIDTH + EPS)
    scale = jnp.broadcast_to(scale, (128, 128)).T
    gain = g_ref[0:1, :]
    for k in range(4):
        cols = slice(k * 128, (k + 1) * 128)
        out_ref[:, cols] = (stream_ref[:, cols] * scale * gain[:, cols]).astype(BF16)


def shifted(array, axis, step):
    size = lax.axis_size(axis)
    return lax.ppermute(array, axis, [(i, (i + step) % size) for i in range(size)])


def exchanged(array, axis):
    return lax.all_to_all(array, axis, 0, 0, tiled=True)


def moved(array, axis, step=1):
    return shifted(array, axis, step)


def layer(
    hidden_in,
    span_order,
    norm_gain,
    w_query,
    bias_query,
    key_value_weight,
    bias_kv,
    w_out,
    post_gain,
):
    z, x, c = (lax.axis_index(a) for a in SEQ)
    own = z * 8 + x * 2 + c

    (w_own,) = call(
        stack_weights,
        [((64, 1280), BF16)],
        w_query,
        key_value_weight,
        w_out.T,
        far=(0, 1, 2),
    )
    w_other = moved(w_own, "c")
    (pieces,) = call(
        prepare, [((NX * NY, 136, 128), BF16)], hidden_in, norm_gain, far=(0, 1)
    )
    arrived = exchanged(pieces, ("x", "tq", "tr"))
    pair = jnp.where(
        c == 0, jnp.concatenate([w_own, w_other], 0), jnp.concatenate([w_other, w_own], 0)
    )
    ring = []
    for k in range(NZ):
        ring += [(k * 2, ((k + 1) % NZ) * 2), (k * 2 + 1, ((k + NZ - 1) % NZ) * 2 + 1)]
    held, wo_own = [pair[:, :768]], pair[:, 768:]
    for _ in range(3):
        held.append(lax.ppermute(held[-1], ("z", "c"), ring))
    same = same_parity()
    swap, one, two, last = [], [], [], []
    for k in range(NZ):
        t = k & 1
        swap.append((k * 2 + 1 - t, k * 2 + t))
        for core, sign in ((0, 1), (1, -1)):
            near, far = (k + sign) % NZ, (k + 2 * sign) % NZ
            one.append(((k * 2 + core) * 2 + t, (near * 2 + core) * 2 + t))
            two.append((k * 2 + core, far * 2 + core))
            if core == 1:
                last.append(((k * 2 + core) * 2 + t, (far * 2 + core) * 2 + t))
    held.append(lax.ppermute(held[2], ("z", "c"), two))
    wo_other = lax.ppermute(wo_own, ("z", "tr"), swap)
    wo_pair = jnp.where(
        lax.axis_index("tr") == 0,
        jnp.concatenate([wo_own, wo_other], 0),
        jnp.concatenate([wo_other, wo_own], 0),
    )
    wo_near = lax.ppermute(wo_pair, ("z", "c", "tr"), one)
    wo_first = jnp.where(same, wo_pair, wo_near)
    wo_second = lax.ppermute(wo_first, ("z", "c"), two)
    wo_third = lax.ppermute(wo_second, ("z", "c", "tr"), last)
    crossed = [moved(held[k], "c") for k in (1, 2, 3)]
    (projected,) = call(
        project,
        [((NX, 768, 128), BF16)],
        arrived,
        *held,
        *crossed,
        scratch=[pltpu.VMEM((1024, 512), BF16)],
        free=range(1, 9),
    )
    (wo_here,) = call(pick, [((512, 512), BF16)], wo_first, wo_second, wo_third)
    shares = exchanged(projected, "x")

    ids = jnp.arange(span_order.shape[0], dtype=jnp.int32)
    own_span = jnp.sum(jnp.where(ids == own, span_order, 0))
    positions = own_span * TOK + jnp.arange(TOK, dtype=jnp.int32)
    half = HEAD // 2
    inverse = jnp.exp(-math.log(ROPE_BASE) * jnp.arange(half, dtype=F32) / half)
    angles = inverse[:, None] * positions.astype(F32)[None, :]
    (residual,) = call(copied, [((128, 512), F32)], hidden_in, far=(0,))
    (bias,) = call(tables, [((768, 128), F32)], bias_query.reshape(1, 512), bias_kv)
    queries, kv = call(
        rotate,
        [((128, 512), BF16), ((NZ, 256, 128), BF16)],
        shares,
        bias,
        jnp.cos(angles),
        jnp.sin(angles),
    )

    wo_there = moved(wo_here, "c")
    kv_here = exchanged(kv, "z")
    others = [moved(queries, "x", step) for step in (1, -1, 2)]
    wo_x = [wo_here] + [moved(wo_here, "x", step) for step in (1, -1, 2)]
    (widened,) = call(copied, [((1, 512), F32)], post_gain.reshape(1, 512))
    kv_there = moved(kv_here, "c")
    (partial,) = call(
        attend,
        [((NX, 144, 512), BF16)],
        span_order,
        queries,
        *others,
        kv_here,
        kv_there,
        scratch=[pltpu.VMEM((2048, 512), F32), pltpu.VMEM((2048, 512), BF16)],
    )
    partial = exchanged(partial, "x")
    wo_c = [wo_there] + [moved(w, "c") for w in wo_x[1:]]
    (gains,) = call(spread, [((8, 512), F32)], widened)
    (attended,) = call(merge, [((512, 128), BF16)], partial)
    attended_other = moved(attended, "tr")
    (out,) = call(
        project_out,
        [((NY // 2, 512, 128), BF16)],
        attended,
        attended_other,
        *wo_x,
        *wo_c,
        scratch=[pltpu.VMEM((2, 512, 128), BF16)],
    )
    out = exchanged(out, "tq")

    attn_out, stream, squares = call(
        mix,
        [((128, 512), BF16), ((128, 512), F32), ((NY, 1, 128), F32)],
        out,
        residual,
        kept=(0,),
    )
    squares = exchanged(squares, TP)
    (normed,) = call(finish, [((128, 512), BF16)], stream, squares, gains, kept=(0,))
    return attn_out, normed


def solution(mesh):
    torus = Mesh(mesh.devices.reshape(NZ, NX, NC, NY // 2, 2), SEQ + TP)
    in_specs = (
        P(SEQ, TP),
        P(),
        P(TP),
        P(SEQ, TP),
        P(TP),
        P(SEQ, None, TP),
        P(None, TP),
        P(TP, SEQ),
        P(TP),
    )
    out_specs = (P(SEQ, TP), P(SEQ, TP))
    return jax.shard_map(
        layer, mesh=torus, in_specs=in_specs, out_specs=out_specs, check_vma=False
    )
```

profile of v0, /device:TPU:6, one launch (start us, length us, event | category | flops | bytes accessed | tf_op | source)
XLA Modules:
  0.0 217.8 jit_solution(15415635701573045201)
XLA Ops:
  2.7 10.2 %all-to-all-start = ((bf16[32,136,128]{2,1,0:T(8,128)(2,1)}), bf16[32,136,128]{2,1,0:T(8,128)(2,1)S(1)}, u32[]{:S(2)}, u32[]{:S(2)}) async-start(bf16[32,136,128]{2,1,0:T(8,128)(2,1)} %shard_map.104), calls=%async_computation | async-start | bytes 2228224 | tf_op jit(solution)/shard_map/all_to_all | solution.py:291
  17.3 4.3 %collective-permute-start.1 = (bf16[128,768]{1,0:T(8,128)(2,1)S(1)}, bf16[128,768]{1,0:T(8,128)(2,1)S(1)}, u32[]{:S(2)}, u32[]{:S(2)}) collective-permute-start(bf16[128,768]{1,0:T(8,128)(2,1)S(1)} %slice.8.refs_0_), channel_id=1, source_target_pairs={{0,64},{8,456},{64,128},{72,8},{128,192},{136,72},{192,256},{200,1... | collective-permute-start | bytes 589832 | tf_op jit(solution)/shard_map/ppermute | solution.py:333
  21.6 10.3 %collective-permute-done.1.refs_1_ = bf16[128,768]{1,0:T(8,128)(2,1)S(1)} collective-permute-done((bf16[128,768]{1,0:T(8,128)(2,1)S(1)}, bf16[128,768]{1,0:T(8,128)(2,1)S(1)}, u32[]{:S(2)}, u32[]{:S(2)}) %collective-permute-start.1) | collective-permute-done | bytes 196640 | tf_op jit(solution)/shard_map/ppermute | solution.py:333
  33.8 6.8 %collective-permute-done.2.refs_2_ = bf16[128,768]{1,0:T(8,128)(2,1)S(1)} collective-permute-done((bf16[128,768]{1,0:T(8,128)(2,1)S(1)}, bf16[128,768]{1,0:T(8,128)(2,1)S(1)}, u32[]{:S(2)}, u32[]{:S(2)}) %collective-permute-start.2) | collective-permute-done | bytes 196640 | tf_op jit(solution)/shard_map/ppermute | solution.py:333
  42.6 3.3 %collective-permute-start.5 = (bf16[128,768]{1,0:T(8,128)(2,1)S(1)}, bf16[128,768]{1,0:T(8,128)(2,1)S(1)}, u32[]{:S(2)}, u32[]{:S(2)}) collective-permute-start(bf16[128,768]{1,0:T(8,128)(2,1)S(1)} %collective-permute-done.1.refs_1_), channel_id=1, source_target_pairs={{0,8},{8,0},{1,9},{9,1},{2,10},{10,2},{3,11},{11,3},{4,12},{12,4},... | collective-permute-start | bytes 589832 | tf_op jit(solution)/shard_map/ppermute | solution.py:287
  47.8 3.0 %collective-permute-start.6 = (bf16[128,768]{1,0:T(8,128)(2,1)S(1)}, bf16[128,768]{1,0:T(8,128)(2,1)S(1)}, u32[]{:S(2)}, u32[]{:S(2)}) collective-permute-start(bf16[128,768]{1,0:T(8,128)(2,1)S(1)} %collective-permute-done.2.refs_2_), channel_id=1, source_target_pairs={{0,8},{8,0},{1,9},{9,1},{2,10},{10,2},{3,11},{11,3},{4,12},{12,4},... | collective-permute-start | bytes 589832 | tf_op jit(solution)/shard_map/ppermute | solution.py:287
  52.8 4.9 %collective-permute-done.4.refs_4_ = bf16[128,768]{1,0:T(8,128)(2,1)S(1)} collective-permute-done((bf16[128,768]{1,0:T(8,128)(2,1)S(1)}, bf16[128,768]{1,0:T(8,128)(2,1)S(1)}, u32[]{:S(2)}, u32[]{:S(2)}) %collective-permute-start.4) | collective-permute-done | bytes 196640 | tf_op jit(solution)/shard_map/ppermute | solution.py:345
  59.7 4.7 %all-to-all-start.1 = ((bf16[4,768,128]{2,1,0:T(8,128)(2,1)}), bf16[4,768,128]{2,1,0:T(8,128)(2,1)S(1)}, u32[]{:S(2)}, u32[]{:S(2)}) async-start(bf16[4,768,128]{2,1,0:T(8,128)(2,1)} %shard_map.106), calls=%async_computation.1 | async-start | bytes 1572864 | tf_op jit(solution)/shard_map/all_to_all | solution.py:291
  67.0 4.9 %collective-permute-done.13 = bf16[128,512]{1,0:T(8,128)(2,1)S(1)} collective-permute-done((bf16[128,512]{1,0:T(8,128)(2,1)S(1)}, bf16[128,512]{1,0:T(8,128)(2,1)S(1)}, u32[]{:S(2)}, u32[]{:S(2)}) %collective-permute-start.13) | collective-permute-done | bytes 131104 | tf_op jit(solution)/shard_map/ppermute | solution.py:346
  74.7 3.5 %all-to-all-start.2 = ((bf16[8,256,128]{2,1,0:T(8,128)(2,1)}), bf16[8,256,128]{2,1,0:T(8,128)(2,1)S(1)}, u32[]{:S(2)}, u32[]{:S(2)}) async-start(bf16[8,256,128]{2,1,0:T(8,128)(2,1)} %get-tuple-element.8), calls=%async_computation.2 | async-start | bytes 1048576 | tf_op jit(solution)/shard_map/all_to_all | solution.py:291
  78.3 4.8 %collective-permute-start.15 = (bf16[256,512]{1,0:T(8,128)(2,1)S(1)}, bf16[256,512]{1,0:T(8,128)(2,1)S(1)}, u32[]{:S(2)}, u32[]{:S(2)}) collective-permute-start(bf16[256,512]{1,0:T(8,128)(2,1)S(1)} %broadcast_select_fusion.h1), channel_id=1, source_target_pairs={{0,128},{8,392},{64,192},{72,456},{128,256},{136,8},{192,320},{200... | collective-permute-start | bytes 786440 | tf_op jit(solution)/shard_map/ppermute | solution.py:354
  83.1 17.1 %collective-permute-done.15.h2 = bf16[256,512]{1,0:T(8,128)(2,1)S(1)} collective-permute-done((bf16[256,512]{1,0:T(8,128)(2,1)S(1)}, bf16[256,512]{1,0:T(8,128)(2,1)S(1)}, u32[]{:S(2)}, u32[]{:S(2)}) %collective-permute-start.15) | collective-permute-done | bytes 262176 | tf_op jit(solution)/shard_map/ppermute | solution.py:354
  102.9 3.4 %collective-permute-start.17 = (bf16[512,512]{1,0:T(8,128)(2,1)S(1)}, bf16[512,512]{1,0:T(8,128)(2,1)S(1)}, u32[]{:S(2)}, u32[]{:S(2)}) collective-permute-start(bf16[512,512]{1,0:T(8,128)(2,1)S(1)} %shard_map.111.refs_0_), channel_id=1, source_target_pairs={{0,16},{16,32},{32,48},{48,0},{1,17},{17,33},{33,49},{49,1},{2,18}... | collective-permute-start | bytes 1572872 | tf_op jit(solution)/shard_map/ppermute | solution.py:287
  106.2 2.5 %collective-permute-start.18 = (bf16[512,512]{1,0:T(8,128)(2,1)S(1)}, bf16[512,512]{1,0:T(8,128)(2,1)S(1)}, u32[]{:S(2)}, u32[]{:S(2)}) collective-permute-start(bf16[512,512]{1,0:T(8,128)(2,1)S(1)} %shard_map.111.refs_0_), channel_id=1, source_target_pairs={{0,48},{16,0},{32,16},{48,32},{1,49},{17,1},{33,17},{49,33},{2,50}... | collective-permute-start | bytes 1572872 | tf_op jit(solution)/shard_map/ppermute | solution.py:287
  108.7 3.4 %collective-permute-start.19 = (bf16[512,512]{1,0:T(8,128)(2,1)S(1)}, bf16[512,512]{1,0:T(8,128)(2,1)S(1)}, u32[]{:S(2)}, u32[]{:S(2)}) collective-permute-start(bf16[512,512]{1,0:T(8,128)(2,1)S(1)} %shard_map.111.refs_0_), channel_id=1, source_target_pairs={{0,32},{16,48},{32,0},{48,16},{1,33},{17,49},{33,1},{49,17},{2,34}... | collective-permute-start | bytes 1572872 | tf_op jit(solution)/shard_map/ppermute | solution.py:287
  112.1 4.0 %collective-permute-start.8 = (bf16[128,512]{1,0:T(8,128)(2,1)S(1)}, bf16[128,512]{1,0:T(8,128)(2,1)S(1)}, u32[]{:S(2)}, u32[]{:S(2)}) collective-permute-start(bf16[128,512]{1,0:T(8,128)(2,1)S(1)} %get-tuple-element.7.q0), channel_id=1, source_target_pairs={{0,16},{16,32},{32,48},{48,0},{1,17},{17,33},{33,49},{49,1},{2,18}... | collective-permute-start | bytes 393224 | tf_op jit(solution)/shard_map/ppermute | solution.py:287
  116.1 15.5 %collective-permute-done.8.q1 = bf16[128,512]{1,0:T(8,128)(2,1)S(1)} collective-permute-done((bf16[128,512]{1,0:T(8,128)(2,1)S(1)}, bf16[128,512]{1,0:T(8,128)(2,1)S(1)}, u32[]{:S(2)}, u32[]{:S(2)}) %collective-permute-start.8) | collective-permute-done | bytes 131104 | tf_op jit(solution)/shard_map/ppermute | solution.py:287
  131.6 3.5 %collective-permute-start.9 = (bf16[128,512]{1,0:T(8,128)(2,1)S(1)}, bf16[128,512]{1,0:T(8,128)(2,1)S(1)}, u32[]{:S(2)}, u32[]{:S(2)}) collective-permute-start(bf16[128,512]{1,0:T(8,128)(2,1)S(1)} %get-tuple-element.7.q0), channel_id=1, source_target_pairs={{0,48},{16,0},{32,16},{48,32},{1,49},{17,1},{33,17},{49,33},{2,50}... | collective-permute-start | bytes 393224 | tf_op jit(solution)/shard_map/ppermute | solution.py:287
  135.1 5.0 %collective-permute-done.9.q2 = bf16[128,512]{1,0:T(8,128)(2,1)S(1)} collective-permute-done((bf16[128,512]{1,0:T(8,128)(2,1)S(1)}, bf16[128,512]{1,0:T(8,128)(2,1)S(1)}, u32[]{:S(2)}, u32[]{:S(2)}) %collective-permute-start.9) | collective-permute-done | bytes 131104 | tf_op jit(solution)/shard_map/ppermute | solution.py:287
  140.1 2.8 %collective-permute-start.10 = (bf16[128,512]{1,0:T(8,128)(2,1)S(1)}, bf16[128,512]{1,0:T(8,128)(2,1)S(1)}, u32[]{:S(2)}, u32[]{:S(2)}) collective-permute-start(bf16[128,512]{1,0:T(8,128)(2,1)S(1)} %get-tuple-element.7.q0), channel_id=1, source_target_pairs={{0,32},{16,48},{32,0},{48,16},{1,33},{17,49},{33,1},{49,17},{2,34}... | collective-permute-start | bytes 393224 | tf_op jit(solution)/shard_map/ppermute | solution.py:287
  143.0 6.7 %collective-permute-done.10.q3 = bf16[128,512]{1,0:T(8,128)(2,1)S(1)} collective-permute-done((bf16[128,512]{1,0:T(8,128)(2,1)S(1)}, bf16[128,512]{1,0:T(8,128)(2,1)S(1)}, u32[]{:S(2)}, u32[]{:S(2)}) %collective-permute-start.10) | collective-permute-done | bytes 131104 | tf_op jit(solution)/shard_map/ppermute | solution.py:287
  149.7 8.5 %shard_map.109 = bf16[4,144,512]{2,1,0:T(8,128)(2,1)} custom-call(s32[64]{0:T(128)S(1)} %copy-done.1, bf16[128,512]{1,0:T(8,128)(2,1)S(1)} %get-tuple-element.7.q0, bf16[128,512]{1,0:T(8,128)(2,1)S(1)} %collective-permute-done.8.q1, bf16[128,512]{1,0:T(8,128)(2,1)S(1)} %collective-permute-done.9.q2, bf16[128,512]{1,0:T(8,128)(2,1)S(1)} %collective-permute-done.10.q3, ...), custom_call_target="tpu_custom_call" | custom-call | tf_op jit(solution)/shard_map/pallas_call | solution.py:43
  158.2 4.5 %all-to-all-start.3 = ((bf16[4,144,512]{2,1,0:T(8,128)(2,1)}), bf16[4,144,512]{2,1,0:T(8,128)(2,1)S(1)}, u32[]{:S(2)}, u32[]{:S(2)}) async-start(bf16[4,144,512]{2,1,0:T(8,128)(2,1)} %shard_map.109), calls=%async_computation.3 | async-start | bytes 1179648 | tf_op jit(solution)/shard_map/all_to_all | solution.py:291
  164.6 2.4 %collective-permute-start.21 = (bf16[512,512]{1,0:T(8,128)(2,1)S(1)}, bf16[512,512]{1,0:T(8,128)(2,1)}, u32[]{:S(2)}, u32[]{:S(2)}) collective-permute-start(bf16[512,512]{1,0:T(8,128)(2,1)S(1)} %collective-permute-done.17.refs_1_), channel_id=1, source_target_pairs={{0,8},{8,0},{1,9},{9,1},{2,10},{10,2},{3,11},{11,3},{4,12},{12,4},... | collective-permute-start | bytes 1572872 | tf_op jit(solution)/shard_map/ppermute | solution.py:287
  169.0 2.4 %collective-permute-start.23 = (bf16[512,512]{1,0:T(8,128)(2,1)S(1)}, bf16[512,512]{1,0:T(8,128)(2,1)}, u32[]{:S(2)}, u32[]{:S(2)}) collective-permute-start(bf16[512,512]{1,0:T(8,128)(2,1)S(1)} %collective-permute-done.19.refs_3_), channel_id=1, source_target_pairs={{0,8},{8,0},{1,9},{9,1},{2,10},{10,2},{3,11},{11,3},{4,12},{12,4},... | collective-permute-start | bytes 1572872 | tf_op jit(solution)/shard_map/ppermute | solution.py:287
  171.6 3.7 %collective-permute-start.12 = (bf16[512,128]{1,0:T(8,128)(2,1)S(1)}, bf16[512,128]{1,0:T(8,128)(2,1)S(1)}, u32[]{:S(2)}, u32[]{:S(2)}) collective-permute-start(bf16[512,128]{1,0:T(8,128)(2,1)S(1)} %shard_map.110.a_own), channel_id=1, source_target_pairs={{0,1},{1,0},{2,3},{3,2},{4,5},{5,4},{6,7},{7,6},{8,9},{9,8},{10,11... | collective-permute-start | bytes 393224 | tf_op jit(solution)/shard_map/ppermute | solution.py:287
  175.3 3.6 %collective-permute-done.12.a_other = bf16[512,128]{1,0:T(8,128)(2,1)S(1)} collective-permute-done((bf16[512,128]{1,0:T(8,128)(2,1)S(1)}, bf16[512,128]{1,0:T(8,128)(2,1)S(1)}, u32[]{:S(2)}, u32[]{:S(2)}) %collective-permute-start.12) | collective-permute-done | bytes 131104 | tf_op jit(solution)/shard_map/ppermute | solution.py:287
  178.9 3.4 %shard_map.112 = bf16[4,512,128]{2,1,0:T(8,128)(2,1)} custom-call(bf16[512,128]{1,0:T(8,128)(2,1)S(1)} %shard_map.110.a_own, bf16[512,128]{1,0:T(8,128)(2,1)S(1)} %collective-permute-done.12.a_other, bf16[512,512]{1,0:T(8,128)(2,1)S(1)} %shard_map.111.refs_0_, bf16[512,512]{1,0:T(8,128)(2,1)S(1)} %collective-permute-done.17.refs_1_, ...), custom_call_target="tpu_custom_call" | custom-call | tf_op jit(solution)/shard_map/pallas_call | solution.py:43
  182.4 7.5 %all-to-all-start.4 = ((bf16[4,512,128]{2,1,0:T(8,128)(2,1)}), bf16[4,512,128]{2,1,0:T(8,128)(2,1)S(1)}, u32[]{:S(2)}, u32[]{:S(2)}) async-start(bf16[4,512,128]{2,1,0:T(8,128)(2,1)} %shard_map.112), calls=%async_computation.4 | async-start | bytes 1048576 | tf_op jit(solution)/shard_map/all_to_all | solution.py:291
  190.8 13.5 %all-to-all-done.4.part_ref = bf16[4,512,128]{2,1,0:T(8,128)(2,1)S(1)} async-done(((bf16[4,512,128]{2,1,0:T(8,128)(2,1)}), bf16[4,512,128]{2,1,0:T(8,128)(2,1)S(1)}, u32[]{:S(2)}, u32[]{:S(2)}) %all-to-all-start.4) | async-done | bytes 524320 | tf_op jit(solution)/shard_map/all_to_all | solution.py:291
  205.2 4.2 %all-to-all-start.5 = ((f32[8,1,128]{2,1,0:T(1,128)}), f32[8,1,128]{2,1,0:T(1,128)S(1)}, u32[]{:S(2)}, u32[]{:S(2)}) async-start(f32[8,1,128]{2,1,0:T(1,128)} %get-tuple-element.11), calls=%async_computation.5 | async-start | bytes 8192 | tf_op jit(solution)/shard_map/all_to_all | solution.py:291
  209.4 7.6 %all-to-all-done.5.sq_ref = f32[8,1,128]{2,1,0:T(1,128)S(1)} async-done(((f32[8,1,128]{2,1,0:T(1,128)}), f32[8,1,128]{2,1,0:T(1,128)S(1)}, u32[]{:S(2)}, u32[]{:S(2)}) %all-to-all-start.5) | async-done | bytes 4128 | tf_op jit(solution)/shard_map/all_to_all | solution.py:291
  (61 shorter events, 30.0 us)
Async XLA Ops:
  2.7 54.9 %all-to-all-start = ((bf16[32,136,128]{2,1,0:T(8,128)(2,1)}), bf16[32,136,128]{2,1,0:T(8,128)(2,1)S(1)}, u32[]{:S(2)}, u32[]{:S(2)}) async-start(bf16[32,136,128]{2,1,0:T(8,128)(2,1)} %shard_map.104), calls=%async_computation | async-start | bytes 2228224 | tf_op jit(solution)/shard_map/all_to_all | solution.py:291
  13.9 3.3 %collective-permute-start = (bf16[64,1280]{1,0:T(8,128)(2,1)S(1)}, bf16[64,1280]{1,0:T(8,128)(2,1)S(1)}, u32[]{:S(2)}, u32[]{:S(2)}) collective-permute-start(bf16[64,1280]{1,0:T(8,128)(2,1)S(1)} %shard_map.105), channel_id=1, source_target_pairs={{0,8},{8,0},{1,9},{9,1},{2,10},{10,2},{3,11},{11,3},{4,12},{12,4},... | collective-permute-start | bytes 491528 | tf_op jit(solution)/shard_map/ppermute | solution.py:287
  17.3 14.6 %collective-permute-start.1 = (bf16[128,768]{1,0:T(8,128)(2,1)S(1)}, bf16[128,768]{1,0:T(8,128)(2,1)S(1)}, u32[]{:S(2)}, u32[]{:S(2)}) collective-permute-start(bf16[128,768]{1,0:T(8,128)(2,1)S(1)} %slice.8.refs_0_), channel_id=1, source_target_pairs={{0,64},{8,456},{64,128},{72,8},{128,192},{136,72},{192,256},{200,1... | collective-permute-start | bytes 589832 | tf_op jit(solution)/shard_map/ppermute | solution.py:333
  31.9 8.8 %collective-permute-start.2 = (bf16[128,768]{1,0:T(8,128)(2,1)S(1)}, bf16[128,768]{1,0:T(8,128)(2,1)S(1)}, u32[]{:S(2)}, u32[]{:S(2)}) collective-permute-start(bf16[128,768]{1,0:T(8,128)(2,1)S(1)} %collective-permute-done.1.refs_1_), channel_id=1, source_target_pairs={{0,64},{8,456},{64,128},{72,8},{128,192},{136,72},{192,256},{200,1... | collective-permute-start | bytes 589832 | tf_op jit(solution)/shard_map/ppermute | solution.py:333
  40.7 10.2 %collective-permute-start.3 = (bf16[128,768]{1,0:T(8,128)(2,1)S(1)}, bf16[128,768]{1,0:T(8,128)(2,1)S(1)}, u32[]{:S(2)}, u32[]{:S(2)}) collective-permute-start(bf16[128,768]{1,0:T(8,128)(2,1)S(1)} %collective-permute-done.2.refs_2_), channel_id=1, source_target_pairs={{0,64},{8,456},{64,128},{72,8},{128,192},{136,72},{192,256},{200,1... | collective-permute-start | bytes 589832 | tf_op jit(solution)/shard_map/ppermute | solution.py:333
  42.6 10.2 %collective-permute-start.5 = (bf16[128,768]{1,0:T(8,128)(2,1)S(1)}, bf16[128,768]{1,0:T(8,128)(2,1)S(1)}, u32[]{:S(2)}, u32[]{:S(2)}) collective-permute-start(bf16[128,768]{1,0:T(8,128)(2,1)S(1)} %collective-permute-done.1.refs_1_), channel_id=1, source_target_pairs={{0,8},{8,0},{1,9},{9,1},{2,10},{10,2},{3,11},{11,3},{4,12},{12,4},... | collective-permute-start | bytes 589832 | tf_op jit(solution)/shard_map/ppermute | solution.py:287
  45.9 11.8 %collective-permute-start.4 = (bf16[128,768]{1,0:T(8,128)(2,1)S(1)}, bf16[128,768]{1,0:T(8,128)(2,1)S(1)}, u32[]{:S(2)}, u32[]{:S(2)}) collective-permute-start(bf16[128,768]{1,0:T(8,128)(2,1)S(1)} %collective-permute-done.2.refs_2_), channel_id=1, source_target_pairs={{0,128},{8,392},{64,192},{72,456},{128,256},{136,8},{192,320},{200... | collective-permute-start | bytes 589832 | tf_op jit(solution)/shard_map/ppermute | solution.py:345
  47.8 9.9 %collective-permute-start.6 = (bf16[128,768]{1,0:T(8,128)(2,1)S(1)}, bf16[128,768]{1,0:T(8,128)(2,1)S(1)}, u32[]{:S(2)}, u32[]{:S(2)}) collective-permute-start(bf16[128,768]{1,0:T(8,128)(2,1)S(1)} %collective-permute-done.2.refs_2_), channel_id=1, source_target_pairs={{0,8},{8,0},{1,9},{9,1},{2,10},{10,2},{3,11},{11,3},{4,12},{12,4},... | collective-permute-start | bytes 589832 | tf_op jit(solution)/shard_map/ppermute | solution.py:287
  50.8 6.8 %collective-permute-start.7 = (bf16[128,768]{1,0:T(8,128)(2,1)S(1)}, bf16[128,768]{1,0:T(8,128)(2,1)S(1)}, u32[]{:S(2)}, u32[]{:S(2)}) collective-permute-start(bf16[128,768]{1,0:T(8,128)(2,1)S(1)} %collective-permute-done.3.refs_3_), channel_id=1, source_target_pairs={{0,8},{8,0},{1,9},{9,1},{2,10},{10,2},{3,11},{11,3},{4,12},{12,4},... | collective-permute-start | bytes 589832 | tf_op jit(solution)/shard_map/ppermute | solution.py:287
  59.7 13.8 %copy-start = (bf16[2,128]{1,0:T(2,128)(2,1)S(1)}, bf16[2,128]{1,0:T(2,128)(2,1)}, u32[]{:S(2)}) copy-start(bf16[2,128]{1,0:T(2,128)(2,1)} %bkv_ref.1) | copy-start | bytes 1540
  59.7 14.0 %all-to-all-start.1 = ((bf16[4,768,128]{2,1,0:T(8,128)(2,1)}), bf16[4,768,128]{2,1,0:T(8,128)(2,1)S(1)}, u32[]{:S(2)}, u32[]{:S(2)}) async-start(bf16[4,768,128]{2,1,0:T(8,128)(2,1)} %shard_map.106), calls=%async_computation.1 | async-start | bytes 1572864 | tf_op jit(solution)/shard_map/all_to_all | solution.py:291
  65.1 6.9 %collective-permute-start.13 = (bf16[128,512]{1,0:T(8,128)(2,1)S(1)}, bf16[128,512]{1,0:T(8,128)(2,1)S(1)}, u32[]{:S(2)}, u32[]{:S(2)}) collective-permute-start(bf16[128,512]{1,0:T(8,128)(2,1)S(1)} %slice.9), channel_id=1, source_target_pairs={{1,0},{64,65},{129,128},{192,193},{257,256},{320,321},{385,384},{4... | collective-permute-start | bytes 393224 | tf_op jit(solution)/shard_map/ppermute | solution.py:346
  72.0 6.3 %collective-permute-start.14 = (bf16[256,512]{1,0:T(8,128)(2,1)S(1)}, bf16[256,512]{1,0:T(8,128)(2,1)S(1)}, u32[]{:S(2)}, u32[]{:S(2)}) collective-permute-start(bf16[256,512]{1,0:T(8,128)(2,1)S(1)} %maximum_select_fusion.1), channel_id=1, source_target_pairs={{0,64},{8,456},{65,129},{73,9},{128,192},{136,72},{193,257},{201,1... | collective-permute-start | bytes 786440 | tf_op jit(solution)/shard_map/ppermute | solution.py:352
  74.7 26.2 %all-to-all-start.2 = ((bf16[8,256,128]{2,1,0:T(8,128)(2,1)}), bf16[8,256,128]{2,1,0:T(8,128)(2,1)S(1)}, u32[]{:S(2)}, u32[]{:S(2)}) async-start(bf16[8,256,128]{2,1,0:T(8,128)(2,1)} %get-tuple-element.8), calls=%async_computation.2 | async-start | bytes 1048576 | tf_op jit(solution)/shard_map/all_to_all | solution.py:291
  78.3 21.9 %collective-permute-start.15 = (bf16[256,512]{1,0:T(8,128)(2,1)S(1)}, bf16[256,512]{1,0:T(8,128)(2,1)S(1)}, u32[]{:S(2)}, u32[]{:S(2)}) collective-permute-start(bf16[256,512]{1,0:T(8,128)(2,1)S(1)} %broadcast_select_fusion.h1), channel_id=1, source_target_pairs={{0,128},{8,392},{64,192},{72,456},{128,256},{136,8},{192,320},{200... | collective-permute-start | bytes 786440 | tf_op jit(solution)/shard_map/ppermute | solution.py:354
  100.2 2.6 %collective-permute-start.16 = (bf16[256,512]{1,0:T(8,128)(2,1)S(1)}, bf16[256,512]{1,0:T(8,128)(2,1)S(1)}, u32[]{:S(2)}, u32[]{:S(2)}) collective-permute-start(bf16[256,512]{1,0:T(8,128)(2,1)S(1)} %collective-permute-done.15.h2), channel_id=1, source_target_pairs={{8,392},{73,457},{136,8},{201,73},{264,136},{329,201},{392,264},{4... | collective-permute-start | bytes 786440 | tf_op jit(solution)/shard_map/ppermute | solution.py:355
  100.9 48.8 %collective-permute-start.11 = (bf16[8,256,128]{2,1,0:T(8,128)(2,1)S(1)}, bf16[8,256,128]{2,1,0:T(8,128)(2,1)S(1)}, u32[]{:S(2)}, u32[]{:S(2)}) collective-permute-start(bf16[8,256,128]{2,1,0:T(8,128)(2,1)S(1)} %all-to-all-done.2.kv0), channel_id=1, source_target_pairs={{0,8},{8,0},{1,9},{9,1},{2,10},{10,2},{3,11},{11,3},{4,12},{12,4},... | collective-permute-start | bytes 1572872 | tf_op jit(solution)/shard_map/ppermute | solution.py:287
  102.9 61.7 %collective-permute-start.17 = (bf16[512,512]{1,0:T(8,128)(2,1)S(1)}, bf16[512,512]{1,0:T(8,128)(2,1)S(1)}, u32[]{:S(2)}, u32[]{:S(2)}) collective-permute-start(bf16[512,512]{1,0:T(8,128)(2,1)S(1)} %shard_map.111.refs_0_), channel_id=1, source_target_pairs={{0,16},{16,32},{32,48},{48,0},{1,17},{17,33},{33,49},{49,1},{2,18}... | collective-permute-start | bytes 1572872 | tf_op jit(solution)/shard_map/ppermute | solution.py:287
  106.2 60.8 %collective-permute-start.18 = (bf16[512,512]{1,0:T(8,128)(2,1)S(1)}, bf16[512,512]{1,0:T(8,128)(2,1)S(1)}, u32[]{:S(2)}, u32[]{:S(2)}) collective-permute-start(bf16[512,512]{1,0:T(8,128)(2,1)S(1)} %shard_map.111.refs_0_), channel_id=1, source_target_pairs={{0,48},{16,0},{32,16},{48,32},{1,49},{17,1},{33,17},{49,33},{2,50}... | collective-permute-start | bytes 1572872 | tf_op jit(solution)/shard_map/ppermute | solution.py:287
  108.7 60.2 %collective-permute-start.19 = (bf16[512,512]{1,0:T(8,128)(2,1)S(1)}, bf16[512,512]{1,0:T(8,128)(2,1)S(1)}, u32[]{:S(2)}, u32[]{:S(2)}) collective-permute-start(bf16[512,512]{1,0:T(8,128)(2,1)S(1)} %shard_map.111.refs_0_), channel_id=1, source_target_pairs={{0,32},{16,48},{32,0},{48,16},{1,33},{17,49},{33,1},{49,17},{2,34}... | collective-permute-start | bytes 1572872 | tf_op jit(solution)/shard_map/ppermute | solution.py:287
  112.1 19.5 %collective-permute-start.8 = (bf16[128,512]{1,0:T(8,128)(2,1)S(1)}, bf16[128,512]{1,0:T(8,128)(2,1)S(1)}, u32[]{:S(2)}, u32[]{:S(2)}) collective-permute-start(bf16[128,512]{1,0:T(8,128)(2,1)S(1)} %get-tuple-element.7.q0), channel_id=1, source_target_pairs={{0,16},{16,32},{32,48},{48,0},{1,17},{17,33},{33,49},{49,1},{2,18}... | collective-permute-start | bytes 393224 | tf_op jit(solution)/shard_map/ppermute | solution.py:287
  131.6 8.5 %collective-permute-start.9 = (bf16[128,512]{1,0:T(8,128)(2,1)S(1)}, bf16[128,512]{1,0:T(8,128)(2,1)S(1)}, u32[]{:S(2)}, u32[]{:S(2)}) collective-permute-start(bf16[128,512]{1,0:T(8,128)(2,1)S(1)} %get-tuple-element.7.q0), channel_id=1, source_target_pairs={{0,48},{16,0},{32,16},{48,32},{1,49},{17,1},{33,17},{49,33},{2,50}... | collective-permute-start | bytes 393224 | tf_op jit(solution)/shard_map/ppermute | solution.py:287
  140.1 9.5 %collective-permute-start.10 = (bf16[128,512]{1,0:T(8,128)(2,1)S(1)}, bf16[128,512]{1,0:T(8,128)(2,1)S(1)}, u32[]{:S(2)}, u32[]{:S(2)}) collective-permute-start(bf16[128,512]{1,0:T(8,128)(2,1)S(1)} %get-tuple-element.7.q0), channel_id=1, source_target_pairs={{0,32},{16,48},{32,0},{48,16},{1,33},{17,49},{33,1},{49,17},{2,34}... | collective-permute-start | bytes 393224 | tf_op jit(solution)/shard_map/ppermute | solution.py:287
  158.2 13.2 %all-to-all-start.3 = ((bf16[4,144,512]{2,1,0:T(8,128)(2,1)}), bf16[4,144,512]{2,1,0:T(8,128)(2,1)S(1)}, u32[]{:S(2)}, u32[]{:S(2)}) async-start(bf16[4,144,512]{2,1,0:T(8,128)(2,1)} %shard_map.109), calls=%async_computation.3 | async-start | bytes 1179648 | tf_op jit(solution)/shard_map/all_to_all | solution.py:291
  162.7 12.6 %collective-permute-start.20 = (bf16[512,512]{1,0:T(8,128)(2,1)S(1)}, bf16[512,512]{1,0:T(8,128)(2,1)S(1)}, u32[]{:S(2)}, u32[]{:S(2)}) collective-permute-start(bf16[512,512]{1,0:T(8,128)(2,1)S(1)} %shard_map.111.refs_0_), channel_id=1, source_target_pairs={{0,8},{8,0},{1,9},{9,1},{2,10},{10,2},{3,11},{11,3},{4,12},{12,4},... | collective-permute-start | bytes 1572872 | tf_op jit(solution)/shard_map/ppermute | solution.py:287
  164.6 10.7 %collective-permute-start.21 = (bf16[512,512]{1,0:T(8,128)(2,1)S(1)}, bf16[512,512]{1,0:T(8,128)(2,1)}, u32[]{:S(2)}, u32[]{:S(2)}) collective-permute-start(bf16[512,512]{1,0:T(8,128)(2,1)S(1)} %collective-permute-done.17.refs_1_), channel_id=1, source_target_pairs={{0,8},{8,0},{1,9},{9,1},{2,10},{10,2},{3,11},{11,3},{4,12},{12,4},... | collective-permute-start | bytes 1572872 | tf_op jit(solution)/shard_map/ppermute | solution.py:287
  167.0 8.2 %collective-permute-start.22 = (bf16[512,512]{1,0:T(8,128)(2,1)S(1)}, bf16[512,512]{1,0:T(8,128)(2,1)}, u32[]{:S(2)}, u32[]{:S(2)}) collective-permute-start(bf16[512,512]{1,0:T(8,128)(2,1)S(1)} %collective-permute-done.18.refs_2_), channel_id=1, source_target_pairs={{0,8},{8,0},{1,9},{9,1},{2,10},{10,2},{3,11},{11,3},{4,12},{12,4},... | collective-permute-start | bytes 1572872 | tf_op jit(solution)/shard_map/ppermute | solution.py:287
  169.0 6.3 %collective-permute-start.23 = (bf16[512,512]{1,0:T(8,128)(2,1)S(1)}, bf16[512,512]{1,0:T(8,128)(2,1)}, u32[]{:S(2)}, u32[]{:S(2)}) collective-permute-start(bf16[512,512]{1,0:T(8,128)(2,1)S(1)} %collective-permute-done.19.refs_3_), channel_id=1, source_target_pairs={{0,8},{8,0},{1,9},{9,1},{2,10},{10,2},{3,11},{11,3},{4,12},{12,4},... | collective-permute-start | bytes 1572872 | tf_op jit(solution)/shard_map/ppermute | solution.py:287
  171.6 7.3 %collective-permute-start.12 = (bf16[512,128]{1,0:T(8,128)(2,1)S(1)}, bf16[512,128]{1,0:T(8,128)(2,1)S(1)}, u32[]{:S(2)}, u32[]{:S(2)}) collective-permute-start(bf16[512,128]{1,0:T(8,128)(2,1)S(1)} %shard_map.110.a_own), channel_id=1, source_target_pairs={{0,1},{1,0},{2,3},{3,2},{4,5},{5,4},{6,7},{7,6},{8,9},{9,8},{10,11... | collective-permute-start | bytes 393224 | tf_op jit(solution)/shard_map/ppermute | solution.py:287
  182.3 27.0 %copy-start.3 = (bf16[512]{0:T(512)(128)(2,1)S(1)}, bf16[512]{0:T(512)(128)(2,1)}, u32[]{:S(2)}) copy-start(bf16[512]{0:T(512)(128)(2,1)} %param.17) | copy-start | bytes 3076
  182.4 22.0 %all-to-all-start.4 = ((bf16[4,512,128]{2,1,0:T(8,128)(2,1)}), bf16[4,512,128]{2,1,0:T(8,128)(2,1)S(1)}, u32[]{:S(2)}, u32[]{:S(2)}) async-start(bf16[4,512,128]{2,1,0:T(8,128)(2,1)} %shard_map.112), calls=%async_computation.4 | async-start | bytes 1048576 | tf_op jit(solution)/shard_map/all_to_all | solution.py:291
  205.2 11.8 %all-to-all-start.5 = ((f32[8,1,128]{2,1,0:T(1,128)}), f32[8,1,128]{2,1,0:T(1,128)S(1)}, u32[]{:S(2)}, u32[]{:S(2)}) async-start(f32[8,1,128]{2,1,0:T(1,128)} %get-tuple-element.11), calls=%async_computation.5 | async-start | bytes 8192 | tf_op jit(solution)/shard_map/all_to_all | solution.py:291
  (2 other events, 18.6 us)
where the time goes:
time: 219 us; the launch traced here: 218 us
  waiting for transfers between devices  97.3 us (44%)
  starting transfers between devices  96.7 us (44%)
  Pallas kernels  20.9 us (10%)
    ppermute x16, starting transfers between devices, shifted(): lax.ppermute(array, axis, [(i, (i + step) % size) for i in range(size)])  43.9 us
    all_to_all x6, starting transfers between devices, exchanged(): return lax.all_to_all(array, axis, 0, 0, tiled=True)  34.7 us
    ppermute x16, waiting for transfers between devices, shifted(): lax.ppermute(array, axis, [(i, (i + step) % size) for i in range(size)])  32.2 us
    all_to_all x6, waiting for transfers between devices, exchanged(): return lax.all_to_all(array, axis, 0, 0, tiled=True)  21.1 us
    pallas_call x14, Pallas kernels, call(): pl.pallas_call(kernel, out_shape=shapes, in_specs=specs, out_specs=spec,...  20.9 us
    ppermute x3, waiting for transfers between devices, layer(): held.append(lax.ppermute(held[-1], ('z', 'c'), ring))  17.1 us
    ppermute x1, waiting for transfers between devices, layer(): wo_second = lax.ppermute(wo_first, ('z', 'c'), two)  17.1 us
    ppermute x3, starting transfers between devices, layer(): held.append(lax.ppermute(held[-1], ('z', 'c'), ring))  8.1 us
  transfers between devices with their start and end apart: 30, of which 12 were waited for; matrix products, arithmetic and copies ran while one was open for 0% of the time, Pallas kernels for 5%

commit v1 on v0

--- a/solution.py
+++ b/solution.py
@@ -220,32 +220,38 @@
         a_ref[head * 128 : (head + 1) * 128, :] = out[:, head * 128 : (head + 1) * 128]
 
 
-def project_out(a_own, a_other, *refs):
-    w_refs, (out_ref, a_ref) = refs[:8], refs[8:]
+def half_rows(w_refs, side):
+    rows = []
+    for w in w_refs:
+        for n in range(2):
+            rows.append(w[pl.ds(pl.multiple_of(n * 256 + side * 128, 128), 128), :])
+    return jnp.concatenate(rows, axis=0)
+
+
+def project_half(a_own, *refs):
+    w_refs, sum_ref = refs[:8], refs[8]
+    sum_ref[...] = jnp.dot(
+        half_rows(w_refs, lax.axis_index("tr")), a_own[...], preferred_element_type=F32
+    )
+
+
+def project_out(sum_ref, a_other, *refs):
+    w_refs, out_ref = refs[:8], refs[8]
     z, x, c = (lax.axis_index(a) for a in SEQ)
-    side = lax.axis_index("tr")
-    a_ref[pl.ds(side, 1)] = a_own[...][None]
-    a_ref[pl.ds(1 - side, 1)] = a_other[...][None]
-    attended = a_ref[...].reshape(1024, 128)
     same = jnp.where(same_parity(), 1, 0)
     low, high = z - 1 + same, z + 1 + same
+    part = jnp.dot(
+        half_rows(w_refs, 1 - lax.axis_index("tr")), a_other[...], preferred_element_type=F32
+    )
+    part = (sum_ref[...] + part).astype(BF16)
     for core in range(2):
-        rows = []
-        for k in range(4):
-            w = w_refs[core * 4 + k]
-            for n in range(2):
-                at = n * 256
-                rows.append(jnp.concatenate([w[at : at + 128, :], w[at + 128 : at + 256, :]], axis=1))
-        part = jnp.dot(
-            jnp.concatenate(rows, axis=0), attended, preferred_element_type=F32
-        ).astype(BF16)
         for k in range(4):
             owner = (x + (0, 3, 1, 2)[k]) & 3
             cols = pl.ds(pl.multiple_of(owner * 128, 128), 128)
             for n in range(2):
                 block = jnp.where(c == core, low - 2 * n, high + 2 * n)
                 y = ((block + NZ) & (NZ - 1)) >> 1
-                at = (k * 2 + n) * 128
+                at = (core * 8 + k * 2 + n) * 128
                 out_ref[pl.ds(y, 1), cols, :] = part[at : at + 128, :][None]
 
 
@@ -404,14 +410,17 @@
     (gains,) = call(spread, [((8, 512), F32)], widened)
     (attended,) = call(merge, [((512, 128), BF16)], partial)
     attended_other = moved(attended, "tr")
+    (half,) = call(
+        project_half, [((2048, 128), F32)], attended, *wo_x, *wo_c, free=range(1, 9)
+    )
     (out,) = call(
         project_out,
         [((NY // 2, 512, 128), BF16)],
-        attended,
+        half,
         attended_other,
         *wo_x,
         *wo_c,
-        scratch=[pltpu.VMEM((2, 512, 128), BF16)],
+        free=range(2, 10),
     )
     out = exchanged(out, "tq")
 

time: 219 us -> 219 us (level)
    pallas_call x14 -> x15, Pallas kernels: 20.9 us -> 22.4 us  [call(): pl.pallas_call(kernel, out_shape=shapes, in_specs=specs, out_specs=spec,...]
  transfers between devices with their start and end apart: 30 -> 30, of which waited for: 12 -> 12; matrix products, arithmetic and copies ran while one was open for 0% -> 0% of each run, Pallas kernels for 5% -> 6%
where the time goes in v1:
time: 219 us; the launch traced here: 217 us
  starting transfers between devices  96.7 us (44%)
  waiting for transfers between devices  95.3 us (44%)
  Pallas kernels  22.4 us (10%)
    ppermute x16, starting transfers between devices, shifted(): lax.ppermute(array, axis, [(i, (i + step) % size) for i in range(size)])  43.9 us
    all_to_all x6, starting transfers between devices, exchanged(): return lax.all_to_all(array, axis, 0, 0, tiled=True)  34.7 us
    ppermute x16, waiting for transfers between devices, shifted(): lax.ppermute(array, axis, [(i, (i + step) % size) for i in range(size)])  30.1 us
    pallas_call x15, Pallas kernels, call(): pl.pallas_call(kernel, out_shape=shapes, in_specs=specs, out_specs=spec,...  22.4 us
    all_to_all x6, waiting for transfers between devices, exchanged(): return lax.all_to_all(array, axis, 0, 0, tiled=True)  21.1 us
    ppermute x3, waiting for transfers between devices, layer(): held.append(lax.ppermute(held[-1], ('z', 'c'), ring))  17.1 us
    ppermute x1, waiting for transfers between devices, layer(): wo_second = lax.ppermute(wo_first, ('z', 'c'), two)  17.1 us
    ppermute x3, starting transfers between devices, layer(): held.append(lax.ppermute(held[-1], ('z', 'c'), ring))  8.1 us
  transfers between devices with their start and end apart: 30, of which 12 were waited for; matrix products, arithmetic and copies ran while one was open for 0% of the time, Pallas kernels for 6%

profile of v1, /device:TPU:6, one launch (start us, length us, event | category | flops | bytes accessed | tf_op | source)
XLA Modules:
  0.0 217.2 jit_solution(14821336408805479659)
XLA Ops:
  0.6 2.1 shard_map.104
  2.7 10.2 %all-to-all-start = ((bf16[32,136,128]{2,1,0:T(8,128)(2,1)}), bf16[32,136,128]{2,1,0:T(8,128)(2,1)S(1)}, u32[]{:S(2)}, u32[]{:S(2)}) async-start(bf16[32,136,128]{2,1,0:T(8,128)(2,1)} %shard_map.104), calls=%async_computation | async-start | bytes 2228224 | tf_op jit(solution)/shard_map/all_to_all | solution.py:297
  17.3 4.3 %collective-permute-start.1 = (bf16[128,768]{1,0:T(8,128)(2,1)S(1)}, bf16[128,768]{1,0:T(8,128)(2,1)S(1)}, u32[]{:S(2)}, u32[]{:S(2)}) collective-permute-start(bf16[128,768]{1,0:T(8,128)(2,1)S(1)} %slice.8.refs_0_), channel_id=1, source_target_pairs={{0,64},{8,456},{64,128},{72,8},{128,192},{136,72},{192,256},{200,1... | collective-permute-start | bytes 589832 | tf_op jit(solution)/shard_map/ppermute | solution.py:339
  21.6 10.3 %collective-permute-done.1.refs_1_ = bf16[128,768]{1,0:T(8,128)(2,1)S(1)} collective-permute-done((bf16[128,768]{1,0:T(8,128)(2,1)S(1)}, bf16[128,768]{1,0:T(8,128)(2,1)S(1)}, u32[]{:S(2)}, u32[]{:S(2)}) %collective-permute-start.1) | collective-permute-done | bytes 196640 | tf_op jit(solution)/shard_map/ppermute | solution.py:339
  33.8 6.8 %collective-permute-done.2.refs_2_ = bf16[128,768]{1,0:T(8,128)(2,1)S(1)} collective-permute-done((bf16[128,768]{1,0:T(8,128)(2,1)S(1)}, bf16[128,768]{1,0:T(8,128)(2,1)S(1)}, u32[]{:S(2)}, u32[]{:S(2)}) %collective-permute-start.2) | collective-permute-done | bytes 196640 | tf_op jit(solution)/shard_map/ppermute | solution.py:339
  42.6 3.3 %collective-permute-start.5 = (bf16[128,768]{1,0:T(8,128)(2,1)S(1)}, bf16[128,768]{1,0:T(8,128)(2,1)S(1)}, u32[]{:S(2)}, u32[]{:S(2)}) collective-permute-start(bf16[128,768]{1,0:T(8,128)(2,1)S(1)} %collective-permute-done.1.refs_1_), channel_id=1, source_target_pairs={{0,8},{8,0},{1,9},{9,1},{2,10},{10,2},{3,11},{11,3},{4,12},{12,4},... | collective-permute-start | bytes 589832 | tf_op jit(solution)/shard_map/ppermute | solution.py:293
  47.8 3.0 %collective-permute-start.6 = (bf16[128,768]{1,0:T(8,128)(2,1)S(1)}, bf16[128,768]{1,0:T(8,128)(2,1)S(1)}, u32[]{:S(2)}, u32[]{:S(2)}) collective-permute-start(bf16[128,768]{1,0:T(8,128)(2,1)S(1)} %collective-permute-done.2.refs_2_), channel_id=1, source_target_pairs={{0,8},{8,0},{1,9},{9,1},{2,10},{10,2},{3,11},{11,3},{4,12},{12,4},... | collective-permute-start | bytes 589832 | tf_op jit(solution)/shard_map/ppermute | solution.py:293
  52.8 4.9 %collective-permute-done.4.refs_4_ = bf16[128,768]{1,0:T(8,128)(2,1)S(1)} collective-permute-done((bf16[128,768]{1,0:T(8,128)(2,1)S(1)}, bf16[128,768]{1,0:T(8,128)(2,1)S(1)}, u32[]{:S(2)}, u32[]{:S(2)}) %collective-permute-start.4) | collective-permute-done | bytes 196640 | tf_op jit(solution)/shard_map/ppermute | solution.py:351
  59.7 4.7 %all-to-all-start.1 = ((bf16[4,768,128]{2,1,0:T(8,128)(2,1)}), bf16[4,768,128]{2,1,0:T(8,128)(2,1)S(1)}, u32[]{:S(2)}, u32[]{:S(2)}) async-start(bf16[4,768,128]{2,1,0:T(8,128)(2,1)} %shard_map.106), calls=%async_computation.1 | async-start | bytes 1572864 | tf_op jit(solution)/shard_map/all_to_all | solution.py:297
  67.0 4.9 %collective-permute-done.12 = bf16[128,512]{1,0:T(8,128)(2,1)S(1)} collective-permute-done((bf16[128,512]{1,0:T(8,128)(2,1)S(1)}, bf16[128,512]{1,0:T(8,128)(2,1)S(1)}, u32[]{:S(2)}, u32[]{:S(2)}) %collective-permute-start.12) | collective-permute-done | bytes 131104 | tf_op jit(solution)/shard_map/ppermute | solution.py:352
  74.7 3.5 %all-to-all-start.2 = ((bf16[8,256,128]{2,1,0:T(8,128)(2,1)}), bf16[8,256,128]{2,1,0:T(8,128)(2,1)S(1)}, u32[]{:S(2)}, u32[]{:S(2)}) async-start(bf16[8,256,128]{2,1,0:T(8,128)(2,1)} %get-tuple-element.8), calls=%async_computation.2 | async-start | bytes 1048576 | tf_op jit(solution)/shard_map/all_to_all | solution.py:297
  78.3 4.8 %collective-permute-start.14 = (bf16[256,512]{1,0:T(8,128)(2,1)S(1)}, bf16[256,512]{1,0:T(8,128)(2,1)S(1)}, u32[]{:S(2)}, u32[]{:S(2)}) collective-permute-start(bf16[256,512]{1,0:T(8,128)(2,1)S(1)} %broadcast_select_fusion.h1), channel_id=1, source_target_pairs={{0,128},{8,392},{64,192},{72,456},{128,256},{136,8},{192,320},{200... | collective-permute-start | bytes 786440 | tf_op jit(solution)/shard_map/ppermute | solution.py:360
  83.1 17.1 %collective-permute-done.14.h2 = bf16[256,512]{1,0:T(8,128)(2,1)S(1)} collective-permute-done((bf16[256,512]{1,0:T(8,128)(2,1)S(1)}, bf16[256,512]{1,0:T(8,128)(2,1)S(1)}, u32[]{:S(2)}, u32[]{:S(2)}) %collective-permute-start.14) | collective-permute-done | bytes 262176 | tf_op jit(solution)/shard_map/ppermute | solution.py:360
  102.9 3.4 %collective-permute-start.16 = (bf16[512,512]{1,0:T(8,128)(2,1)S(1)}, bf16[512,512]{1,0:T(8,128)(2,1)S(1)}, u32[]{:S(2)}, u32[]{:S(2)}) collective-permute-start(bf16[512,512]{1,0:T(8,128)(2,1)S(1)} %shard_map.111.refs_0_), channel_id=1, source_target_pairs={{0,16},{16,32},{32,48},{48,0},{1,17},{17,33},{33,49},{49,1},{2,18}... | collective-permute-start | bytes 1572872 | tf_op jit(solution)/shard_map/ppermute | solution.py:293
  106.2 2.5 %collective-permute-start.17 = (bf16[512,512]{1,0:T(8,128)(2,1)S(1)}, bf16[512,512]{1,0:T(8,128)(2,1)S(1)}, u32[]{:S(2)}, u32[]{:S(2)}) collective-permute-start(bf16[512,512]{1,0:T(8,128)(2,1)S(1)} %shard_map.111.refs_0_), channel_id=1, source_target_pairs={{0,48},{16,0},{32,16},{48,32},{1,49},{17,1},{33,17},{49,33},{2,50}... | collective-permute-start | bytes 1572872 | tf_op jit(solution)/shard_map/ppermute | solution.py:293
  108.7 3.4 %collective-permute-start.18 = (bf16[512,512]{1,0:T(8,128)(2,1)S(1)}, bf16[512,512]{1,0:T(8,128)(2,1)S(1)}, u32[]{:S(2)}, u32[]{:S(2)}) collective-permute-start(bf16[512,512]{1,0:T(8,128)(2,1)S(1)} %shard_map.111.refs_0_), channel_id=1, source_target_pairs={{0,32},{16,48},{32,0},{48,16},{1,33},{17,49},{33,1},{49,17},{2,34}... | collective-permute-start | bytes 1572872 | tf_op jit(solution)/shard_map/ppermute | solution.py:293
  112.1 4.0 %collective-permute-start.8 = (bf16[128,512]{1,0:T(8,128)(2,1)S(1)}, bf16[128,512]{1,0:T(8,128)(2,1)S(1)}, u32[]{:S(2)}, u32[]{:S(2)}) collective-permute-start(bf16[128,512]{1,0:T(8,128)(2,1)S(1)} %get-tuple-element.7.q0), channel_id=1, source_target_pairs={{0,16},{16,32},{32,48},{48,0},{1,17},{17,33},{33,49},{49,1},{2,18}... | collective-permute-start | bytes 393224 | tf_op jit(solution)/shard_map/ppermute | solution.py:293
  116.1 15.5 %collective-permute-done.8.q1 = bf16[128,512]{1,0:T(8,128)(2,1)S(1)} collective-permute-done((bf16[128,512]{1,0:T(8,128)(2,1)S(1)}, bf16[128,512]{1,0:T(8,128)(2,1)S(1)}, u32[]{:S(2)}, u32[]{:S(2)}) %collective-permute-start.8) | collective-permute-done | bytes 131104 | tf_op jit(solution)/shard_map/ppermute | solution.py:293
  131.6 3.5 %collective-permute-start.9 = (bf16[128,512]{1,0:T(8,128)(2,1)S(1)}, bf16[128,512]{1,0:T(8,128)(2,1)S(1)}, u32[]{:S(2)}, u32[]{:S(2)}) collective-permute-start(bf16[128,512]{1,0:T(8,128)(2,1)S(1)} %get-tuple-element.7.q0), channel_id=1, source_target_pairs={{0,48},{16,0},{32,16},{48,32},{1,49},{17,1},{33,17},{49,33},{2,50}... | collective-permute-start | bytes 393224 | tf_op jit(solution)/shard_map/ppermute | solution.py:293
  135.1 5.0 %collective-permute-done.9.q2 = bf16[128,512]{1,0:T(8,128)(2,1)S(1)} collective-permute-done((bf16[128,512]{1,0:T(8,128)(2,1)S(1)}, bf16[128,512]{1,0:T(8,128)(2,1)S(1)}, u32[]{:S(2)}, u32[]{:S(2)}) %collective-permute-start.9) | collective-permute-done | bytes 131104 | tf_op jit(solution)/shard_map/ppermute | solution.py:293
  140.1 2.8 %collective-permute-start.10 = (bf16[128,512]{1,0:T(8,128)(2,1)S(1)}, bf16[128,512]{1,0:T(8,128)(2,1)S(1)}, u32[]{:S(2)}, u32[]{:S(2)}) collective-permute-start(bf16[128,512]{1,0:T(8,128)(2,1)S(1)} %get-tuple-element.7.q0), channel_id=1, source_target_pairs={{0,32},{16,48},{32,0},{48,16},{1,33},{17,49},{33,1},{49,17},{2,34}... | collective-permute-start | bytes 393224 | tf_op jit(solution)/shard_map/ppermute | solution.py:293
  143.0 6.7 %collective-permute-done.10.q3 = bf16[128,512]{1,0:T(8,128)(2,1)S(1)} collective-permute-done((bf16[128,512]{1,0:T(8,128)(2,1)S(1)}, bf16[128,512]{1,0:T(8,128)(2,1)S(1)}, u32[]{:S(2)}, u32[]{:S(2)}) %collective-permute-start.10) | collective-permute-done | bytes 131104 | tf_op jit(solution)/shard_map/ppermute | solution.py:293
  149.7 8.5 %shard_map.109 = bf16[4,144,512]{2,1,0:T(8,128)(2,1)} custom-call(s32[64]{0:T(128)S(1)} %copy-done.1, bf16[128,512]{1,0:T(8,128)(2,1)S(1)} %get-tuple-element.7.q0, bf16[128,512]{1,0:T(8,128)(2,1)S(1)} %collective-permute-done.8.q1, bf16[128,512]{1,0:T(8,128)(2,1)S(1)} %collective-permute-done.9.q2, bf16[128,512]{1,0:T(8,128)(2,1)S(1)} %collective-permute-done.10.q3, ...), custom_call_target="tpu_custom_call" | custom-call | tf_op jit(solution)/shard_map/pallas_call | solution.py:43
  158.2 4.5 %all-to-all-start.3 = ((bf16[4,144,512]{2,1,0:T(8,128)(2,1)}), bf16[4,144,512]{2,1,0:T(8,128)(2,1)S(1)}, u32[]{:S(2)}, u32[]{:S(2)}) async-start(bf16[4,144,512]{2,1,0:T(8,128)(2,1)} %shard_map.109), calls=%async_computation.3 | async-start | bytes 1179648 | tf_op jit(solution)/shard_map/all_to_all | solution.py:297
  164.6 2.4 %collective-permute-start.20 = (bf16[512,512]{1,0:T(8,128)(2,1)S(1)}, bf16[512,512]{1,0:T(8,128)(2,1)}, u32[]{:S(2)}, u32[]{:S(2)}) collective-permute-start(bf16[512,512]{1,0:T(8,128)(2,1)S(1)} %collective-permute-done.16.refs_1_), channel_id=1, source_target_pairs={{0,8},{8,0},{1,9},{9,1},{2,10},{10,2},{3,11},{11,3},{4,12},{12,4},... | collective-permute-start | bytes 1572872 | tf_op jit(solution)/shard_map/ppermute | solution.py:293
  169.0 2.4 %collective-permute-start.22 = (bf16[512,512]{1,0:T(8,128)(2,1)S(1)}, bf16[512,512]{1,0:T(8,128)(2,1)}, u32[]{:S(2)}, u32[]{:S(2)}) collective-permute-start(bf16[512,512]{1,0:T(8,128)(2,1)S(1)} %collective-permute-done.18.refs_3_), channel_id=1, source_target_pairs={{0,8},{8,0},{1,9},{9,1},{2,10},{10,2},{3,11},{11,3},{4,12},{12,4},... | collective-permute-start | bytes 1572872 | tf_op jit(solution)/shard_map/ppermute | solution.py:293
  171.6 3.7 %collective-permute-start.23 = (bf16[512,128]{1,0:T(8,128)(2,1)S(1)}, bf16[512,128]{1,0:T(8,128)(2,1)S(1)}, u32[]{:S(2)}, u32[]{:S(2)}) collective-permute-start(bf16[512,128]{1,0:T(8,128)(2,1)S(1)} %shard_map.110.a_own), channel_id=1, source_target_pairs={{0,1},{1,0},{2,3},{3,2},{4,5},{5,4},{6,7},{7,6},{8,9},{9,8},{10,11... | collective-permute-start | bytes 393224 | tf_op jit(solution)/shard_map/ppermute | solution.py:293
  178.9 2.9 %shard_map.113 = bf16[4,512,128]{2,1,0:T(8,128)(2,1)} custom-call(f32[2048,128]{1,0:T(8,128)S(1)} %shard_map.112.sum_ref, bf16[512,128]{1,0:T(8,128)(2,1)S(1)} %collective-permute-done.23.a_other, bf16[512,512]{1,0:T(8,128)(2,1)S(1)} %shard_map.111.refs_0_, bf16[512,512]{1,0:T(8,128)(2,1)S(1)} %collective-permute-done.16.refs_1_, ...), custom_call_target="tpu_custom_call" | custom-call | tf_op jit(solution)/shard_map/pallas_call | solution.py:43
  181.8 7.6 %all-to-all-start.4 = ((bf16[4,512,128]{2,1,0:T(8,128)(2,1)}), bf16[4,512,128]{2,1,0:T(8,128)(2,1)S(1)}, u32[]{:S(2)}, u32[]{:S(2)}) async-start(bf16[4,512,128]{2,1,0:T(8,128)(2,1)} %shard_map.113), calls=%async_computation.4 | async-start | bytes 1048576 | tf_op jit(solution)/shard_map/all_to_all | solution.py:297
  190.2 13.5 %all-to-all-done.4.part_ref = bf16[4,512,128]{2,1,0:T(8,128)(2,1)S(1)} async-done(((bf16[4,512,128]{2,1,0:T(8,128)(2,1)}), bf16[4,512,128]{2,1,0:T(8,128)(2,1)S(1)}, u32[]{:S(2)}, u32[]{:S(2)}) %all-to-all-start.4) | async-done | bytes 524320 | tf_op jit(solution)/shard_map/all_to_all | solution.py:297
  204.6 4.2 %all-to-all-start.5 = ((f32[8,1,128]{2,1,0:T(1,128)}), f32[8,1,128]{2,1,0:T(1,128)S(1)}, u32[]{:S(2)}, u32[]{:S(2)}) async-start(f32[8,1,128]{2,1,0:T(1,128)} %get-tuple-element.11), calls=%async_computation.5 | async-start | bytes 8192 | tf_op jit(solution)/shard_map/all_to_all | solution.py:297
  208.8 7.6 %all-to-all-done.5.sq_ref = f32[8,1,128]{2,1,0:T(1,128)S(1)} async-done(((f32[8,1,128]{2,1,0:T(1,128)}), f32[8,1,128]{2,1,0:T(1,128)S(1)}, u32[]{:S(2)}, u32[]{:S(2)}) %all-to-all-start.5) | async-done | bytes 4128 | tf_op jit(solution)/shard_map/all_to_all | solution.py:297
  (62 shorter events, 31.6 us)
Async XLA Ops:
  2.7 54.9 %all-to-all-start = ((bf16[32,136,128]{2,1,0:T(8,128)(2,1)}), bf16[32,136,128]{2,1,0:T(8,128)(2,1)S(1)}, u32[]{:S(2)}, u32[]{:S(2)}) async-start(bf16[32,136,128]{2,1,0:T(8,128)(2,1)} %shard_map.104), calls=%async_computation | async-start | bytes 2228224 | tf_op jit(solution)/shard_map/all_to_all | solution.py:297
  13.9 3.3 %collective-permute-start = (bf16[64,1280]{1,0:T(8,128)(2,1)S(1)}, bf16[64,1280]{1,0:T(8,128)(2,1)S(1)}, u32[]{:S(2)}, u32[]{:S(2)}) collective-permute-start(bf16[64,1280]{1,0:T(8,128)(2,1)S(1)} %shard_map.105), channel_id=1, source_target_pairs={{0,8},{8,0},{1,9},{9,1},{2,10},{10,2},{3,11},{11,3},{4,12},{12,4},... | collective-permute-start | bytes 491528 | tf_op jit(solution)/shard_map/ppermute | solution.py:293
  17.3 14.6 %collective-permute-start.1 = (bf16[128,768]{1,0:T(8,128)(2,1)S(1)}, bf16[128,768]{1,0:T(8,128)(2,1)S(1)}, u32[]{:S(2)}, u32[]{:S(2)}) collective-permute-start(bf16[128,768]{1,0:T(8,128)(2,1)S(1)} %slice.8.refs_0_), channel_id=1, source_target_pairs={{0,64},{8,456},{64,128},{72,8},{128,192},{136,72},{192,256},{200,1... | collective-permute-start | bytes 589832 | tf_op jit(solution)/shard_map/ppermute | solution.py:339
  31.9 8.8 %collective-permute-start.2 = (bf16[128,768]{1,0:T(8,128)(2,1)S(1)}, bf16[128,768]{1,0:T(8,128)(2,1)S(1)}, u32[]{:S(2)}, u32[]{:S(2)}) collective-permute-start(bf16[128,768]{1,0:T(8,128)(2,1)S(1)} %collective-permute-done.1.refs_1_), channel_id=1, source_target_pairs={{0,64},{8,456},{64,128},{72,8},{128,192},{136,72},{192,256},{200,1... | collective-permute-start | bytes 589832 | tf_op jit(solution)/shard_map/ppermute | solution.py:339
  40.7 10.2 %collective-permute-start.3 = (bf16[128,768]{1,0:T(8,128)(2,1)S(1)}, bf16[128,768]{1,0:T(8,128)(2,1)S(1)}, u32[]{:S(2)}, u32[]{:S(2)}) collective-permute-start(bf16[128,768]{1,0:T(8,128)(2,1)S(1)} %collective-permute-done.2.refs_2_), channel_id=1, source_target_pairs={{0,64},{8,456},{64,128},{72,8},{128,192},{136,72},{192,256},{200,1... | collective-permute-start | bytes 589832 | tf_op jit(solution)/shard_map/ppermute | solution.py:339
  42.6 10.2 %collective-permute-start.5 = (bf16[128,768]{1,0:T(8,128)(2,1)S(1)}, bf16[128,768]{1,0:T(8,128)(2,1)S(1)}, u32[]{:S(2)}, u32[]{:S(2)}) collective-permute-start(bf16[128,768]{1,0:T(8,128)(2,1)S(1)} %collective-permute-done.1.refs_1_), channel_id=1, source_target_pairs={{0,8},{8,0},{1,9},{9,1},{2,10},{10,2},{3,11},{11,3},{4,12},{12,4},... | collective-permute-start | bytes 589832 | tf_op jit(solution)/shard_map/ppermute | solution.py:293
  45.9 11.8 %collective-permute-start.4 = (bf16[128,768]{1,0:T(8,128)(2,1)S(1)}, bf16[128,768]{1,0:T(8,128)(2,1)S(1)}, u32[]{:S(2)}, u32[]{:S(2)}) collective-permute-start(bf16[128,768]{1,0:T(8,128)(2,1)S(1)} %collective-permute-done.2.refs_2_), channel_id=1, source_target_pairs={{0,128},{8,392},{64,192},{72,456},{128,256},{136,8},{192,320},{200... | collective-permute-start | bytes 589832 | tf_op jit(solution)/shard_map/ppermute | solution.py:351
  47.8 9.9 %collective-permute-start.6 = (bf16[128,768]{1,0:T(8,128)(2,1)S(1)}, bf16[128,768]{1,0:T(8,128)(2,1)S(1)}, u32[]{:S(2)}, u32[]{:S(2)}) collective-permute-start(bf16[128,768]{1,0:T(8,128)(2,1)S(1)} %collective-permute-done.2.refs_2_), channel_id=1, source_target_pairs={{0,8},{8,0},{1,9},{9,1},{2,10},{10,2},{3,11},{11,3},{4,12},{12,4},... | collective-permute-start | bytes 589832 | tf_op jit(solution)/shard_map/ppermute | solution.py:293
  50.8 6.8 %collective-permute-start.7 = (bf16[128,768]{1,0:T(8,128)(2,1)S(1)}, bf16[128,768]{1,0:T(8,128)(2,1)S(1)}, u32[]{:S(2)}, u32[]{:S(2)}) collective-permute-start(bf16[128,768]{1,0:T(8,128)(2,1)S(1)} %collective-permute-done.3.refs_3_), channel_id=1, source_target_pairs={{0,8},{8,0},{1,9},{9,1},{2,10},{10,2},{3,11},{11,3},{4,12},{12,4},... | collective-permute-start | bytes 589832 | tf_op jit(solution)/shard_map/ppermute | solution.py:293
  59.7 13.8 %copy-start = (bf16[2,128]{1,0:T(2,128)(2,1)S(1)}, bf16[2,128]{1,0:T(2,128)(2,1)}, u32[]{:S(2)}) copy-start(bf16[2,128]{1,0:T(2,128)(2,1)} %bkv_ref.1) | copy-start | bytes 1540
  59.7 14.0 %all-to-all-start.1 = ((bf16[4,768,128]{2,1,0:T(8,128)(2,1)}), bf16[4,768,128]{2,1,0:T(8,128)(2,1)S(1)}, u32[]{:S(2)}, u32[]{:S(2)}) async-start(bf16[4,768,128]{2,1,0:T(8,128)(2,1)} %shard_map.106), calls=%async_computation.1 | async-start | bytes 1572864 | tf_op jit(solution)/shard_map/all_to_all | solution.py:297
  65.1 6.9 %collective-permute-start.12 = (bf16[128,512]{1,0:T(8,128)(2,1)S(1)}, bf16[128,512]{1,0:T(8,128)(2,1)S(1)}, u32[]{:S(2)}, u32[]{:S(2)}) collective-permute-start(bf16[128,512]{1,0:T(8,128)(2,1)S(1)} %slice.9), channel_id=1, source_target_pairs={{1,0},{64,65},{129,128},{192,193},{257,256},{320,321},{385,384},{4... | collective-permute-start | bytes 393224 | tf_op jit(solution)/shard_map/ppermute | solution.py:352
  72.0 6.3 %collective-permute-start.13 = (bf16[256,512]{1,0:T(8,128)(2,1)S(1)}, bf16[256,512]{1,0:T(8,128)(2,1)S(1)}, u32[]{:S(2)}, u32[]{:S(2)}) collective-permute-start(bf16[256,512]{1,0:T(8,128)(2,1)S(1)} %maximum_select_fusion.1), channel_id=1, source_target_pairs={{0,64},{8,456},{65,129},{73,9},{128,192},{136,72},{193,257},{201,1... | collective-permute-start | bytes 786440 | tf_op jit(solution)/shard_map/ppermute | solution.py:358
  74.7 26.2 %all-to-all-start.2 = ((bf16[8,256,128]{2,1,0:T(8,128)(2,1)}), bf16[8,256,128]{2,1,0:T(8,128)(2,1)S(1)}, u32[]{:S(2)}, u32[]{:S(2)}) async-start(bf16[8,256,128]{2,1,0:T(8,128)(2,1)} %get-tuple-element.8), calls=%async_computation.2 | async-start | bytes 1048576 | tf_op jit(solution)/shard_map/all_to_all | solution.py:297
  78.3 21.9 %collective-permute-start.14 = (bf16[256,512]{1,0:T(8,128)(2,1)S(1)}, bf16[256,512]{1,0:T(8,128)(2,1)S(1)}, u32[]{:S(2)}, u32[]{:S(2)}) collective-permute-start(bf16[256,512]{1,0:T(8,128)(2,1)S(1)} %broadcast_select_fusion.h1), channel_id=1, source_target_pairs={{0,128},{8,392},{64,192},{72,456},{128,256},{136,8},{192,320},{200... | collective-permute-start | bytes 786440 | tf_op jit(solution)/shard_map/ppermute | solution.py:360
  100.2 2.6 %collective-permute-start.15 = (bf16[256,512]{1,0:T(8,128)(2,1)S(1)}, bf16[256,512]{1,0:T(8,128)(2,1)S(1)}, u32[]{:S(2)}, u32[]{:S(2)}) collective-permute-start(bf16[256,512]{1,0:T(8,128)(2,1)S(1)} %collective-permute-done.14.h2), channel_id=1, source_target_pairs={{8,392},{73,457},{136,8},{201,73},{264,136},{329,201},{392,264},{4... | collective-permute-start | bytes 786440 | tf_op jit(solution)/shard_map/ppermute | solution.py:361
  100.9 48.8 %collective-permute-start.11 = (bf16[8,256,128]{2,1,0:T(8,128)(2,1)S(1)}, bf16[8,256,128]{2,1,0:T(8,128)(2,1)S(1)}, u32[]{:S(2)}, u32[]{:S(2)}) collective-permute-start(bf16[8,256,128]{2,1,0:T(8,128)(2,1)S(1)} %all-to-all-done.2.kv0), channel_id=1, source_target_pairs={{0,8},{8,0},{1,9},{9,1},{2,10},{10,2},{3,11},{11,3},{4,12},{12,4},... | collective-permute-start | bytes 1572872 | tf_op jit(solution)/shard_map/ppermute | solution.py:293
  102.9 61.7 %collective-permute-start.16 = (bf16[512,512]{1,0:T(8,128)(2,1)S(1)}, bf16[512,512]{1,0:T(8,128)(2,1)S(1)}, u32[]{:S(2)}, u32[]{:S(2)}) collective-permute-start(bf16[512,512]{1,0:T(8,128)(2,1)S(1)} %shard_map.111.refs_0_), channel_id=1, source_target_pairs={{0,16},{16,32},{32,48},{48,0},{1,17},{17,33},{33,49},{49,1},{2,18}... | collective-permute-start | bytes 1572872 | tf_op jit(solution)/shard_map/ppermute | solution.py:293
  106.2 60.8 %collective-permute-start.17 = (bf16[512,512]{1,0:T(8,128)(2,1)S(1)}, bf16[512,512]{1,0:T(8,128)(2,1)S(1)}, u32[]{:S(2)}, u32[]{:S(2)}) collective-permute-start(bf16[512,512]{1,0:T(8,128)(2,1)S(1)} %shard_map.111.refs_0_), channel_id=1, source_target_pairs={{0,48},{16,0},{32,16},{48,32},{1,49},{17,1},{33,17},{49,33},{2,50}... | collective-permute-start | bytes 1572872 | tf_op jit(solution)/shard_map/ppermute | solution.py:293
  108.7 60.2 %collective-permute-start.18 = (bf16[512,512]{1,0:T(8,128)(2,1)S(1)}, bf16[512,512]{1,0:T(8,128)(2,1)S(1)}, u32[]{:S(2)}, u32[]{:S(2)}) collective-permute-start(bf16[512,512]{1,0:T(8,128)(2,1)S(1)} %shard_map.111.refs_0_), channel_id=1, source_target_pairs={{0,32},{16,48},{32,0},{48,16},{1,33},{17,49},{33,1},{49,17},{2,34}... | collective-permute-start | bytes 1572872 | tf_op jit(solution)/shard_map/ppermute | solution.py:293
  112.1 19.5 %collective-permute-start.8 = (bf16[128,512]{1,0:T(8,128)(2,1)S(1)}, bf16[128,512]{1,0:T(8,128)(2,1)S(1)}, u32[]{:S(2)}, u32[]{:S(2)}) collective-permute-start(bf16[128,512]{1,0:T(8,128)(2,1)S(1)} %get-tuple-element.7.q0), channel_id=1, source_target_pairs={{0,16},{16,32},{32,48},{48,0},{1,17},{17,33},{33,49},{49,1},{2,18}... | collective-permute-start | bytes 393224 | tf_op jit(solution)/shard_map/ppermute | solution.py:293
  131.6 8.5 %collective-permute-start.9 = (bf16[128,512]{1,0:T(8,128)(2,1)S(1)}, bf16[128,512]{1,0:T(8,128)(2,1)S(1)}, u32[]{:S(2)}, u32[]{:S(2)}) collective-permute-start(bf16[128,512]{1,0:T(8,128)(2,1)S(1)} %get-tuple-element.7.q0), channel_id=1, source_target_pairs={{0,48},{16,0},{32,16},{48,32},{1,49},{17,1},{33,17},{49,33},{2,50}... | collective-permute-start | bytes 393224 | tf_op jit(solution)/shard_map/ppermute | solution.py:293
  140.1 9.5 %collective-permute-start.10 = (bf16[128,512]{1,0:T(8,128)(2,1)S(1)}, bf16[128,512]{1,0:T(8,128)(2,1)S(1)}, u32[]{:S(2)}, u32[]{:S(2)}) collective-permute-start(bf16[128,512]{1,0:T(8,128)(2,1)S(1)} %get-tuple-element.7.q0), channel_id=1, source_target_pairs={{0,32},{16,48},{32,0},{48,16},{1,33},{17,49},{33,1},{49,17},{2,34}... | collective-permute-start | bytes 393224 | tf_op jit(solution)/shard_map/ppermute | solution.py:293
  158.2 13.2 %all-to-all-start.3 = ((bf16[4,144,512]{2,1,0:T(8,128)(2,1)}), bf16[4,144,512]{2,1,0:T(8,128)(2,1)S(1)}, u32[]{:S(2)}, u32[]{:S(2)}) async-start(bf16[4,144,512]{2,1,0:T(8,128)(2,1)} %shard_map.109), calls=%async_computation.3 | async-start | bytes 1179648 | tf_op jit(solution)/shard_map/all_to_all | solution.py:297
  162.7 12.6 %collective-permute-start.19 = (bf16[512,512]{1,0:T(8,128)(2,1)S(1)}, bf16[512,512]{1,0:T(8,128)(2,1)S(1)}, u32[]{:S(2)}, u32[]{:S(2)}) collective-permute-start(bf16[512,512]{1,0:T(8,128)(2,1)S(1)} %shard_map.111.refs_0_), channel_id=1, source_target_pairs={{0,8},{8,0},{1,9},{9,1},{2,10},{10,2},{3,11},{11,3},{4,12},{12,4},... | collective-permute-start | bytes 1572872 | tf_op jit(solution)/shard_map/ppermute | solution.py:293
  164.6 10.7 %collective-permute-start.20 = (bf16[512,512]{1,0:T(8,128)(2,1)S(1)}, bf16[512,512]{1,0:T(8,128)(2,1)}, u32[]{:S(2)}, u32[]{:S(2)}) collective-permute-start(bf16[512,512]{1,0:T(8,128)(2,1)S(1)} %collective-permute-done.16.refs_1_), channel_id=1, source_target_pairs={{0,8},{8,0},{1,9},{9,1},{2,10},{10,2},{3,11},{11,3},{4,12},{12,4},... | collective-permute-start | bytes 1572872 | tf_op jit(solution)/shard_map/ppermute | solution.py:293
  167.0 8.2 %collective-permute-start.21 = (bf16[512,512]{1,0:T(8,128)(2,1)S(1)}, bf16[512,512]{1,0:T(8,128)(2,1)}, u32[]{:S(2)}, u32[]{:S(2)}) collective-permute-start(bf16[512,512]{1,0:T(8,128)(2,1)S(1)} %collective-permute-done.17.refs_2_), channel_id=1, source_target_pairs={{0,8},{8,0},{1,9},{9,1},{2,10},{10,2},{3,11},{11,3},{4,12},{12,4},... | collective-permute-start | bytes 1572872 | tf_op jit(solution)/shard_map/ppermute | solution.py:293
  169.0 6.3 %collective-permute-start.22 = (bf16[512,512]{1,0:T(8,128)(2,1)S(1)}, bf16[512,512]{1,0:T(8,128)(2,1)}, u32[]{:S(2)}, u32[]{:S(2)}) collective-permute-start(bf16[512,512]{1,0:T(8,128)(2,1)S(1)} %collective-permute-done.18.refs_3_), channel_id=1, source_target_pairs={{0,8},{8,0},{1,9},{9,1},{2,10},{10,2},{3,11},{11,3},{4,12},{12,4},... | collective-permute-start | bytes 1572872 | tf_op jit(solution)/shard_map/ppermute | solution.py:293
  171.6 7.3 %collective-permute-start.23 = (bf16[512,128]{1,0:T(8,128)(2,1)S(1)}, bf16[512,128]{1,0:T(8,128)(2,1)S(1)}, u32[]{:S(2)}, u32[]{:S(2)}) collective-permute-start(bf16[512,128]{1,0:T(8,128)(2,1)S(1)} %shard_map.110.a_own), channel_id=1, source_target_pairs={{0,1},{1,0},{2,3},{3,2},{4,5},{5,4},{6,7},{7,6},{8,9},{9,8},{10,11... | collective-permute-start | bytes 393224 | tf_op jit(solution)/shard_map/ppermute | solution.py:293
  181.8 27.0 %copy-start.3 = (bf16[512]{0:T(512)(128)(2,1)S(1)}, bf16[512]{0:T(512)(128)(2,1)}, u32[]{:S(2)}) copy-start(bf16[512]{0:T(512)(128)(2,1)} %param.17) | copy-start | bytes 3076
  181.8 22.0 %all-to-all-start.4 = ((bf16[4,512,128]{2,1,0:T(8,128)(2,1)}), bf16[4,512,128]{2,1,0:T(8,128)(2,1)S(1)}, u32[]{:S(2)}, u32[]{:S(2)}) async-start(bf16[4,512,128]{2,1,0:T(8,128)(2,1)} %shard_map.113), calls=%async_computation.4 | async-start | bytes 1048576 | tf_op jit(solution)/shard_map/all_to_all | solution.py:297
  204.6 11.8 %all-to-all-start.5 = ((f32[8,1,128]{2,1,0:T(1,128)}), f32[8,1,128]{2,1,0:T(1,128)S(1)}, u32[]{:S(2)}, u32[]{:S(2)}) async-start(f32[8,1,128]{2,1,0:T(1,128)} %get-tuple-element.11), calls=%async_computation.5 | async-start | bytes 8192 | tf_op jit(solution)/shard_map/all_to_all | solution.py:297
  (2 other events, 18.6 us)
